TPU v7x, 32 devices: a whole 2x2x4 slice. The times are simulated.
32 devices in a mesh: row: 8 (over y, x, core), col: 4 (over z).
Axes of the slice: x: 2, y: 2, z: 4, core: 2. Of those that a mesh axis runs over, the one named last changes fastest.
Arguments:
- jacobian: float32 [2, 4096, 256], P(None, ('row', 'col')), may hold values from -0.25 to 0.25
Outputs:
- normal_tiles: float32 [8, 2, 4, 512, 512], P('row', None, 'col')
All inputs are finite; a program needn't handle non-finite values.
Results may differ from a plain program's by a relative error of at most 0.0003.
Values sent between devices are 32-bit elements; how exact they have to be, the bound alone decides.
A program may use at most 64 MiB of HBM per device.

v0:
```python
import jax
import jax.numpy as jnp
from jax import lax
from jax.sharding import PartitionSpec as P


def from_partner(block, axis, distance):
    count = lax.axis_size(axis)
    route = []
    for low in range(count):
        high = low | 1 << distance
        if high != low and high < count:
            route += [(low, high), (high, low)]
    return lax.ppermute(block, axis, route)


def partner_rows(block, bit_number):
    return from_partner(block, ("row", "col"), bit_number)


def body(jacobian):
    row_index = lax.axis_index("row")
    col_index = lax.axis_index("col")
    col_count = lax.axis_size("col")
    cycles = lax.axis_size("row") // col_count
    panel_count = jacobian.shape[0]
    width = jacobian.shape[2]
    own_tile = lax.all_gather(jacobian, "col", axis=1, tiled=True)
    tile_size = own_tile.shape[1]
    col_bits = col_count.bit_length() - 1
    low_row = row_index % col_count
    moved = jacobian
    for bit_number in range(col_bits):
        first = partner_rows(moved, bit_number)
        second = partner_rows(first, bit_number + col_bits)
        differ = low_row >> bit_number & 1 != col_index >> bit_number & 1
        moved = jnp.where(differ, second, moved)
    gathered = lax.all_gather(moved, "row", axis=1, tiled=True)
    gathered = gathered.reshape(panel_count, cycles, tile_size, width)
    partners = [gathered[:, turn_index] for turn_index in range(cycles)]

    def product(partner):
        return jnp.einsum("pak,pbk->ab", own_tile, partner, precision=lax.Precision.HIGHEST)

    def empty_tile(partner):
        return jnp.zeros((tile_size, tile_size), jnp.float32)

    results = []
    for turn_index in range(cycles):
        column_tile = col_index + col_count * turn_index
        results.append(
            lax.cond(column_tile <= row_index, product, empty_tile, partners[turn_index])
        )
    blocks = jnp.stack(results, 0)
    return blocks[None, :, None]


def solution(mesh):
    in_specs = (P(None, ("row", "col"), None),)
    out_specs = P("row", None, "col", None, None)
    return jax.shard_map(body, mesh=mesh, in_specs=in_specs, out_specs=out_specs, check_vma=False)
```

profile of v0, /device:TPU:4, one launch (start us, length us, event | category | flops | bytes accessed | tf_op | source)
XLA Modules:
  0.0 115.7 jit_solution(6772489944896085306)
XLA Ops:
  6.5 0.0 all-gather.3.cloned.1.call-start
  6.5 1.6 %collective-permute-start = (f32[2,128,256]{2,1,0:T(8,128)}, f32[2,128,256]{2,1,0:T(8,128)S(1)}, u32[]{:S(2)}, u32[]{:S(2)}) collective-permute-start(f32[2,128,256]{2,1,0:T(8,128)} %param.5), channel_id=1, source_target_pairs={{0,1},{1,0},{2,3},{3,2},{4,5},{5,4},{6,7},{7,6},{8,9},{9,8},{10,11... | collective-permute-start | bytes 786440 | tf_op jit(solution)/shard_map/ppermute | solution.py:14
  8.1 6.7 %collective-permute-done = f32[2,128,256]{2,1,0:T(8,128)S(1)} collective-permute-done((f32[2,128,256]{2,1,0:T(8,128)}, f32[2,128,256]{2,1,0:T(8,128)S(1)}, u32[]{:S(2)}, u32[]{:S(2)}) %collective-permute-start) | collective-permute-done | bytes 262176 | tf_op jit(solution)/shard_map/ppermute | solution.py:14
  14.8 0.0 collective-permute-start.1
  14.8 1.5 %collective-permute-done.1 = f32[2,128,256]{2,1,0:T(8,128)S(1)} collective-permute-done((f32[2,128,256]{2,1,0:T(8,128)S(1)}, f32[2,128,256]{2,1,0:T(8,128)S(1)}, u32[]{:S(2)}, u32[]{:S(2)}) %collective-permute-start.1) | collective-permute-done | bytes 262176 | tf_op jit(solution)/shard_map/ppermute | solution.py:14
  16.3 1.0 broadcast_select_fusion
  17.3 2.7 %collective-permute-start.2 = (f32[2,128,256]{2,1,0:T(8,128)S(1)}, f32[2,128,256]{2,1,0:T(8,128)S(1)}, u32[]{:S(2)}, u32[]{:S(2)}) collective-permute-start(f32[2,128,256]{2,1,0:T(8,128)S(1)} %broadcast_select_fusion), channel_id=1, source_target_pairs={{0,2},{2,0},{1,3},{3,1},{4,6},{6,4},{5,7},{7,5},{8,10},{10,8},{9,1... | collective-permute-start | bytes 786440 | tf_op jit(solution)/shard_map/ppermute | solution.py:14
  20.0 11.3 %collective-permute-done.2 = f32[2,128,256]{2,1,0:T(8,128)S(1)} collective-permute-done((f32[2,128,256]{2,1,0:T(8,128)S(1)}, f32[2,128,256]{2,1,0:T(8,128)S(1)}, u32[]{:S(2)}, u32[]{:S(2)}) %collective-permute-start.2) | collective-permute-done | bytes 262176 | tf_op jit(solution)/shard_map/ppermute | solution.py:14
  31.3 1.5 %collective-permute-start.3 = (f32[2,128,256]{2,1,0:T(8,128)S(1)}, f32[2,128,256]{2,1,0:T(8,128)S(1)}, u32[]{:S(2)}, u32[]{:S(2)}) collective-permute-start(f32[2,128,256]{2,1,0:T(8,128)S(1)} %collective-permute-done.2), channel_id=1, source_target_pairs={{0,8},{8,0},{1,9},{9,1},{2,10},{10,2},{3,11},{11,3},{4,12},{12,4},... | collective-permute-start | bytes 786440 | tf_op jit(solution)/shard_map/ppermute | solution.py:14
  32.8 5.1 %collective-permute-done.3 = f32[2,128,256]{2,1,0:T(8,128)S(1)} collective-permute-done((f32[2,128,256]{2,1,0:T(8,128)S(1)}, f32[2,128,256]{2,1,0:T(8,128)S(1)}, u32[]{:S(2)}, u32[]{:S(2)}) %collective-permute-start.3) | collective-permute-done | bytes 262176 | tf_op jit(solution)/shard_map/ppermute | solution.py:14
  37.8 0.7 broadcast_select_fusion.1
  38.6 0.0 all-gather.3.cloned.1.call-update
  38.6 0.0 all-gather.5.cloned.1.call-start
  38.7 0.7 all-gather.5.cloned.1.call-update
  39.4 30.0 %all-gather.3.cloned.1.call-done = f32[2,1024,256]{2,1,0:T(8,128)} async-done(((f32[2,128,256]{2,1,0:T(8,128)}), f32[2,1024,256]{2,1,0:T(8,128)}) %all-gather.3.cloned.1.call-update) | async-done | bytes 2097168 | tf_op jit(solution)/shard_map/all_gather | solution.py:38
  69.3 1.7 %copy.2 = f32[2,2,512,256]{3,2,0,1:T(8,128)S(1)} copy(f32[2,2,512,256]{3,2,1,0:T(8,128)} %bitcast.17) | data formatting | bytes 4194304 | tf_op jit(solution)/shard_map/cond | solution.py:52
  71.1 27.9 %all-gather.5.cloned.1.call-done = f32[2,512,256]{2,1,0:T(8,128)} async-done(((f32[2,128,256]{2,1,0:T(8,128)}), f32[2,512,256]{2,1,0:T(8,128)}) %all-gather.5.cloned.1.call-update) | async-done | bytes 1048592 | tf_op jit(solution)/shard_map/all_gather | solution.py:28
  99.0 3.1 %conditional.3 = (f32[1,512,512]{2,1,0:T(8,128)S(1)}) conditional(s32[]{:T(128)} %convert_element_type.7, () %tuple.23, (f32[2,2,512,256]{3,2,0,1:T(8,128)S(1)}, f32[2,512,256]{2,1,0:T(8,128)}) %tuple.24), branch_computations={%region_2.3_spmd, %region_3.4_spmd} | conditional | flops 1610612736 | bytes 3145736 | solution.py:52
  99.0 3.1 %convolution_bitcast_fusion.1 = f32[1,512,512]{2,1,0:T(8,128)S(1)} fusion(f32[2,512,256]{2,1,0:T(8,128)} %get-tuple-element.27, f32[2,2,512,256]{3,2,0,1:T(8,128)S(1)} %get-tuple-element.28), kind=kOutput, calls=%fused_computation.3 | convolution fusion | flops 1610612736 | bytes 3145728 | tf_op jit(solution)/shard_map/cond/branch_1_fun/pak,pbk->ab/dot_general | solution.py:43
  102.1 4.1 %conditional.2 = (f32[1,512,512]{2,1,0:T(8,128)}) conditional(s32[]{:T(128)} %convert_element_type.6, () %tuple.21, (f32[2,2,512,256]{3,2,0,1:T(8,128)S(1)}, f32[2,512,256]{2,1,0:T(8,128)}) %tuple.24), branch_computations={%region_0.1_spmd, %region_1.2_spmd} | conditional | flops 1610612736 | bytes 3145736 | solution.py:52
  102.1 4.1 %convolution_bitcast_fusion = f32[1,512,512]{2,1,0:T(8,128)} fusion(f32[2,512,256]{2,1,0:T(8,128)} %get-tuple-element.25, f32[2,2,512,256]{3,2,0,1:T(8,128)S(1)} %get-tuple-element.26), kind=kOutput, calls=%fused_computation | convolution fusion | flops 1610612736 | bytes 3145728 | tf_op jit(solution)/shard_map/cond/branch_1_fun/pak,pbk->ab/dot_general | solution.py:43
  106.2 2.7 %maximum_bitcast_fusion = f32[1,2,1,512,512]{4,3,2,1,0:T(8,128)} fusion(f32[1,512,512]{2,1,0:T(8,128)S(1)} %get-tuple-element.34, f32[1,512,512]{2,1,0:T(8,128)} %get-tuple-element.33), kind=kLoop, calls=%fused_computation.6 | loop fusion | flops 524288 | bytes 4194304 | tf_op jit(solution)/shard_map/broadcast_in_dim | solution.py:55
Async XLA Ops:
  6.5 62.8 %all-gather.3.cloned.1.call-start = ((), (), s32[]{:S(2)}) async-start(), calls=%async_computation | async-start | bytes 2359296 | tf_op jit(solution)/shard_map/all_gather | solution.py:38
  6.5 8.3 %collective-permute-start = (f32[2,128,256]{2,1,0:T(8,128)}, f32[2,128,256]{2,1,0:T(8,128)S(1)}, u32[]{:S(2)}, u32[]{:S(2)}) collective-permute-start(f32[2,128,256]{2,1,0:T(8,128)} %param.5), channel_id=1, source_target_pairs={{0,1},{1,0},{2,3},{3,2},{4,5},{5,4},{6,7},{7,6},{8,9},{9,8},{10,11... | collective-permute-start | bytes 786440 | tf_op jit(solution)/shard_map/ppermute | solution.py:14
  14.8 1.5 %collective-permute-start.1 = (f32[2,128,256]{2,1,0:T(8,128)S(1)}, f32[2,128,256]{2,1,0:T(8,128)S(1)}, u32[]{:S(2)}, u32[]{:S(2)}) collective-permute-start(f32[2,128,256]{2,1,0:T(8,128)S(1)} %collective-permute-done), channel_id=1, source_target_pairs={{0,4},{4,0},{1,5},{5,1},{2,6},{6,2},{3,7},{7,3},{8,12},{12,8},{9,1... | collective-permute-start | bytes 786440 | tf_op jit(solution)/shard_map/ppermute | solution.py:14
  17.3 14.0 %collective-permute-start.2 = (f32[2,128,256]{2,1,0:T(8,128)S(1)}, f32[2,128,256]{2,1,0:T(8,128)S(1)}, u32[]{:S(2)}, u32[]{:S(2)}) collective-permute-start(f32[2,128,256]{2,1,0:T(8,128)S(1)} %broadcast_select_fusion), channel_id=1, source_target_pairs={{0,2},{2,0},{1,3},{3,1},{4,6},{6,4},{5,7},{7,5},{8,10},{10,8},{9,1... | collective-permute-start | bytes 786440 | tf_op jit(solution)/shard_map/ppermute | solution.py:14
  31.3 6.5 %collective-permute-start.3 = (f32[2,128,256]{2,1,0:T(8,128)S(1)}, f32[2,128,256]{2,1,0:T(8,128)S(1)}, u32[]{:S(2)}, u32[]{:S(2)}) collective-permute-start(f32[2,128,256]{2,1,0:T(8,128)S(1)} %collective-permute-done.2), channel_id=1, source_target_pairs={{0,8},{8,0},{1,9},{9,1},{2,10},{10,2},{3,11},{11,3},{4,12},{12,4},... | collective-permute-start | bytes 786440 | tf_op jit(solution)/shard_map/ppermute | solution.py:14
  38.6 60.4 %all-gather.5.cloned.1.call-start = ((), (), s32[]{:S(2)}) async-start(), calls=%async_computation.1 | async-start | bytes 1310720 | tf_op jit(solution)/shard_map/all_gather | solution.py:28
Sparse Core Ops, SparseCore 0:
  38.7 30.5 all-gather.2
  70.9 28.0 all-gather.4
where the time goes:
time: 116 us
  waiting for transfers between devices  83.2 us (72%)
  between operations  13.4 us (12%)
  matrix products  7.14 us (6%)
  starting transfers between devices  5.77 us (5%)
  other arithmetic  4.43 us (4%)
  local copies, waits for them, and re-layouts  1.73 us (1%)
    all_gather x1, waiting for transfers between devices, body(): gathered = lax.all_gather(moved, 'row', axis=1, tiled=True)  30 us
    all_gather x1, waiting for transfers between devices, body(): own_tile = lax.all_gather(jacobian, 'col', axis=1, tiled=True)  27.9 us
    ppermute x4, waiting for transfers between devices, from_partner(): return lax.ppermute(block, axis, route)  24.6 us
    dot_general x2, matrix products, product(): jnp.einsum('pak,pbk->ab', own_tile, partner, precision=lax.Precision.HIGH...  7.14 us
    ppermute x4, starting transfers between devices, from_partner(): return lax.ppermute(block, axis, route)  5.72 us
    broadcast_in_dim x1, other arithmetic, body(): return blocks[None, :, None]  2.71 us
  transfers between devices with their start and end apart: 6, of which 6 were waited for; matrix products, arithmetic and copies ran while one was open for 1% of the time, Pallas kernels for 0%

commit v1 on v0

--- a/solution.py
+++ b/solution.py
@@ -25,7 +25,12 @@
     cycles = lax.axis_size("row") // col_count
     panel_count = jacobian.shape[0]
     width = jacobian.shape[2]
-    own_tile = lax.all_gather(jacobian, "col", axis=1, tiled=True)
+    ring = [jacobian]
+    for hop in range(3):
+        ring.append(lax.ppermute(ring[-1], "col", [(dev, (dev + 1) % 4) for dev in range(4)]))
+    own_tile = jnp.roll(
+        jnp.concatenate(ring[::-1], axis=1), (lax.axis_index("col") + 1) * ring[0].shape[1], axis=1
+    )
     tile_size = own_tile.shape[1]
     col_bits = col_count.bit_length() - 1
     low_row = row_index % col_count

time: 116 us -> 102 us (0.88)
  waiting for transfers between devices: 83.2 us -> 71.6 us
  matrix products: 7.14 us -> 5.7 us
  starting transfers between devices: 5.77 us -> 4.37 us
  local copies, waits for them, and re-layouts: 1.73 us -> 2.89 us
    all_gather x1 -> x0, waiting for transfers between devices: 27.9 us -> none  [body(): own_tile = lax.all_gather(jacobian, 'col', axis=1, tiled=True)]
    ppermute x0 -> x3, waiting for transfers between devices: none -> 25.3 us  [body(): lax.ppermute(ring[-1], 'col', [(dev, (dev + 1) % 4) for dev in range(4)])]
    ppermute x4, waiting for transfers between devices: 24.6 us -> 20.3 us  [from_partner(): return lax.ppermute(block, axis, route)]
    all_gather x1, waiting for transfers between devices: 30 us -> 25.9 us  [body(): gathered = lax.all_gather(moved, 'row', axis=1, tiled=True)]
    ppermute x4, starting transfers between devices: 5.72 us -> 2.79 us  [from_partner(): return lax.ppermute(block, axis, route)]
    ppermute x0 -> x3, starting transfers between devices: none -> 1.58 us  [body(): lax.ppermute(ring[-1], 'col', [(dev, (dev + 1) % 4) for dev in range(4)])]
    dot_general x2, matrix products: 7.14 us -> 5.7 us  [product(): jnp.einsum('pak,pbk->ab', own_tile, partner, precision=lax.Precision.HIGH...]
  transfers between devices with their start and end apart: 6 -> 8, of which waited for: 6 -> 7; matrix products, arithmetic and copies ran while one was open for 1% -> 1% of each run, Pallas kernels for 0% -> 0%
where the time goes in v1:
time: 102 us
  waiting for transfers between devices  71.6 us (70%)
  between operations  13.5 us (13%)
  matrix products  5.7 us (6%)
  starting transfers between devices  4.37 us (4%)
  other arithmetic  3.81 us (4%)
  local copies, waits for them, and re-layouts  2.89 us (3%)
    all_gather x1, waiting for transfers between devices, body(): gathered = lax.all_gather(moved, 'row', axis=1, tiled=True)  25.9 us
    ppermute x3, waiting for transfers between devices, body(): lax.ppermute(ring[-1], 'col', [(dev, (dev + 1) % 4) for dev in range(4)])  25.3 us
    ppermute x4, waiting for transfers between devices, from_partner(): return lax.ppermute(block, axis, route)  20.3 us
    dot_general x2, matrix products, product(): jnp.einsum('pak,pbk->ab', own_tile, partner, precision=lax.Precision.HIGH...  5.7 us
    broadcast_in_dim x1, other arithmetic, body(): return blocks[None, :, None]  3.03 us
    ppermute x4, starting transfers between devices, from_partner(): return lax.ppermute(block, axis, route)  2.79 us
  transfers between devices with their start and end apart: 8, of which 7 were waited for; matrix products, arithmetic and copies ran while one was open for 1% of the time, Pallas kernels for 0%

profile of v1, /device:TPU:4, one launch (start us, length us, event | category | flops | bytes accessed | tf_op | source)
XLA Modules:
  0.0 101.9 jit_solution(9827314079498389836)
XLA Ops:
  6.5 1.6 %collective-permute-start.4 = (f32[2,128,256]{2,1,0:T(8,128)}, f32[2,128,256]{2,1,0:T(8,128)S(1)}, u32[]{:S(2)}, u32[]{:S(2)}) collective-permute-start(f32[2,128,256]{2,1,0:T(8,128)} %param.5), channel_id=1, source_target_pairs={{0,1},{1,2},{2,3},{3,0},{4,5},{5,6},{6,7},{7,4},{8,9},{9,10},{10,1... | collective-permute-start | bytes 786440 | tf_op jit(solution)/shard_map/ppermute | solution.py:30
  8.1 8.6 %collective-permute-done.4 = f32[2,128,256]{2,1,0:T(8,128)S(1)} collective-permute-done((f32[2,128,256]{2,1,0:T(8,128)}, f32[2,128,256]{2,1,0:T(8,128)S(1)}, u32[]{:S(2)}, u32[]{:S(2)}) %collective-permute-start.4) | collective-permute-done | bytes 262176 | tf_op jit(solution)/shard_map/ppermute | solution.py:30
  16.7 0.0 collective-permute-start.5
  16.7 1.2 %collective-permute-start = (f32[2,128,256]{2,1,0:T(8,128)}, f32[2,128,256]{2,1,0:T(8,128)S(1)}, u32[]{:S(2)}, u32[]{:S(2)}) collective-permute-start(f32[2,128,256]{2,1,0:T(8,128)} %param.5), channel_id=1, source_target_pairs={{0,1},{1,0},{2,3},{3,2},{4,5},{5,4},{6,7},{7,6},{8,9},{9,8},{10,11... | collective-permute-start | bytes 786440 | tf_op jit(solution)/shard_map/ppermute | solution.py:14
  17.9 9.7 %collective-permute-done.5 = f32[2,128,256]{2,1,0:T(8,128)S(1)} collective-permute-done((f32[2,128,256]{2,1,0:T(8,128)S(1)}, f32[2,128,256]{2,1,0:T(8,128)S(1)}, u32[]{:S(2)}, u32[]{:S(2)}) %collective-permute-start.5) | collective-permute-done | bytes 262176 | tf_op jit(solution)/shard_map/ppermute | solution.py:30
  27.7 0.0 collective-permute-start.6
  27.7 2.4 %collective-permute-done = f32[2,128,256]{2,1,0:T(8,128)S(1)} collective-permute-done((f32[2,128,256]{2,1,0:T(8,128)}, f32[2,128,256]{2,1,0:T(8,128)S(1)}, u32[]{:S(2)}, u32[]{:S(2)}) %collective-permute-start) | collective-permute-done | bytes 262176 | tf_op jit(solution)/shard_map/ppermute | solution.py:14
  30.1 6.9 %collective-permute-done.6 = f32[2,128,256]{2,1,0:T(8,128)S(1)} collective-permute-done((f32[2,128,256]{2,1,0:T(8,128)S(1)}, f32[2,128,256]{2,1,0:T(8,128)S(1)}, u32[]{:S(2)}, u32[]{:S(2)}) %collective-permute-start.6) | collective-permute-done | bytes 262176 | tf_op jit(solution)/shard_map/ppermute | solution.py:30
  37.2 1.0 constant_dynamic-update-slice_fusion.4
  38.2 0.0 collective-permute-done.1
  38.3 0.1 collective-permute-start.2
  38.4 11.2 %collective-permute-done.2 = f32[2,128,256]{2,1,0:T(8,128)S(1)} collective-permute-done((f32[2,128,256]{2,1,0:T(8,128)S(1)}, f32[2,128,256]{2,1,0:T(8,128)S(1)}, u32[]{:S(2)}, u32[]{:S(2)}) %collective-permute-start.2) | collective-permute-done | bytes 262176 | tf_op jit(solution)/shard_map/ppermute | solution.py:14
  49.5 1.5 %collective-permute-start.3 = (f32[2,128,256]{2,1,0:T(8,128)S(1)}, f32[2,128,256]{2,1,0:T(8,128)S(1)}, u32[]{:S(2)}, u32[]{:S(2)}) collective-permute-start(f32[2,128,256]{2,1,0:T(8,128)S(1)} %collective-permute-done.2), channel_id=1, source_target_pairs={{0,8},{8,0},{1,9},{9,1},{2,10},{10,2},{3,11},{11,3},{4,12},{12,4},... | collective-permute-start | bytes 786440 | tf_op jit(solution)/shard_map/ppermute | solution.py:14
  51.0 6.7 %collective-permute-done.3 = f32[2,128,256]{2,1,0:T(8,128)S(1)} collective-permute-done((f32[2,128,256]{2,1,0:T(8,128)S(1)}, f32[2,128,256]{2,1,0:T(8,128)S(1)}, u32[]{:S(2)}, u32[]{:S(2)}) %collective-permute-start.3) | collective-permute-done | bytes 262176 | tf_op jit(solution)/shard_map/ppermute | solution.py:14
  57.8 0.7 broadcast_select_fusion.1
  58.5 0.0 all-gather.2.cloned.1.call-update
  58.5 0.1 constant_dynamic-slice_fusion
  58.6 25.9 %all-gather.2.cloned.1.call-done = f32[2,1024,256]{2,1,0:T(8,128)} async-done(((f32[2,128,256]{2,1,0:T(8,128)}), f32[2,1024,256]{2,1,0:T(8,128)}) %all-gather.2.cloned.1.call-update) | async-done | bytes 2097168 | tf_op jit(solution)/shard_map/all_gather | solution.py:43
  84.5 1.7 %copy.2 = f32[2,2,512,256]{3,2,0,1:T(8,128)S(1)} copy(f32[2,2,512,256]{3,2,1,0:T(8,128)} %bitcast.17) | data formatting | bytes 4194304 | tf_op jit(solution)/shard_map/cond | solution.py:57
  86.3 2.9 %conditional.3 = (f32[1,512,512]{2,1,0:T(8,128)}) conditional(s32[]{:T(128)} %convert_element_type.7, () %tuple.23, (f32[2,2,512,256]{3,2,0,1:T(8,128)S(1)}, f32[2,512,256]{2,1,0:T(8,128)S(1)}) %tuple.24), branch_computations={%region_2.3_spmd, %region_3.4_spmd} | conditional | flops 1610612736 | bytes 3145736 | solution.py:57
  86.3 2.9 %convolution_bitcast_fusion.1 = f32[1,512,512]{2,1,0:T(8,128)} fusion(f32[2,512,256]{2,1,0:T(8,128)S(1)} %get-tuple-element.27, f32[2,2,512,256]{3,2,0,1:T(8,128)S(1)} %get-tuple-element.28), kind=kOutput, calls=%fused_computation.3 | convolution fusion | flops 1610612736 | bytes 3145728 | tf_op jit(solution)/shard_map/cond/branch_1_fun/pak,pbk->ab/dot_general | solution.py:48
  89.2 2.8 %conditional.2 = (f32[1,512,512]{2,1,0:T(8,128)}) conditional(s32[]{:T(128)} %convert_element_type.6, () %tuple.21, (f32[2,2,512,256]{3,2,0,1:T(8,128)S(1)}, f32[2,512,256]{2,1,0:T(8,128)S(1)}) %tuple.24), branch_computations={%region_0.1_spmd, %region_1.2_spmd} | conditional | flops 1610612736 | bytes 3145736 | solution.py:57
  89.2 2.8 %convolution_bitcast_fusion = f32[1,512,512]{2,1,0:T(8,128)} fusion(f32[2,512,256]{2,1,0:T(8,128)S(1)} %get-tuple-element.25, f32[2,2,512,256]{3,2,0,1:T(8,128)S(1)} %get-tuple-element.26), kind=kOutput, calls=%fused_computation | convolution fusion | flops 1610612736 | bytes 3145728 | tf_op jit(solution)/shard_map/cond/branch_1_fun/pak,pbk->ab/dot_general | solution.py:48
  92.0 3.0 %maximum_bitcast_fusion = f32[1,2,1,512,512]{4,3,2,1,0:T(8,128)} fusion(f32[1,512,512]{2,1,0:T(8,128)} %get-tuple-element.36, f32[1,512,512]{2,1,0:T(8,128)} %get-tuple-element.35), kind=kLoop, calls=%fused_computation.6 | loop fusion | flops 524288 | bytes 4194304 | tf_op jit(solution)/shard_map/broadcast_in_dim | solution.py:60
  (11 shorter events, 0.2 us)
Async XLA Ops:
  6.5 31.7 %copy-start = (f32[2,128,256]{2,1,0:T(8,128)S(1)}, f32[2,128,256]{2,1,0:T(8,128)}, u32[]{:S(2)}) copy-start(f32[2,128,256]{2,1,0:T(8,128)} %param.5) | copy-start | bytes 786436
  6.5 78.0 %all-gather.2.cloned.1.call-start = ((), (), s32[]{:S(2)}) async-start(), calls=%async_computation | async-start | bytes 2359296 | tf_op jit(solution)/shard_map/all_gather | solution.py:43
  6.5 10.2 %collective-permute-start.4 = (f32[2,128,256]{2,1,0:T(8,128)}, f32[2,128,256]{2,1,0:T(8,128)S(1)}, u32[]{:S(2)}, u32[]{:S(2)}) collective-permute-start(f32[2,128,256]{2,1,0:T(8,128)} %param.5), channel_id=1, source_target_pairs={{0,1},{1,2},{2,3},{3,0},{4,5},{5,6},{6,7},{7,4},{8,9},{9,10},{10,1... | collective-permute-start | bytes 786440 | tf_op jit(solution)/shard_map/ppermute | solution.py:30
  16.7 11.0 %collective-permute-start.5 = (f32[2,128,256]{2,1,0:T(8,128)S(1)}, f32[2,128,256]{2,1,0:T(8,128)S(1)}, u32[]{:S(2)}, u32[]{:S(2)}) collective-permute-start(f32[2,128,256]{2,1,0:T(8,128)S(1)} %collective-permute-done.4), channel_id=1, source_target_pairs={{0,1},{1,2},{2,3},{3,0},{4,5},{5,6},{6,7},{7,4},{8,9},{9,10},{10,1... | collective-permute-start | bytes 786440 | tf_op jit(solution)/shard_map/ppermute | solution.py:30
  16.7 13.4 %collective-permute-start = (f32[2,128,256]{2,1,0:T(8,128)}, f32[2,128,256]{2,1,0:T(8,128)S(1)}, u32[]{:S(2)}, u32[]{:S(2)}) collective-permute-start(f32[2,128,256]{2,1,0:T(8,128)} %param.5), channel_id=1, source_target_pairs={{0,1},{1,0},{2,3},{3,2},{4,5},{5,4},{6,7},{7,6},{8,9},{9,8},{10,11... | collective-permute-start | bytes 786440 | tf_op jit(solution)/shard_map/ppermute | solution.py:14
  27.7 9.4 %collective-permute-start.6 = (f32[2,128,256]{2,1,0:T(8,128)S(1)}, f32[2,128,256]{2,1,0:T(8,128)S(1)}, u32[]{:S(2)}, u32[]{:S(2)}) collective-permute-start(f32[2,128,256]{2,1,0:T(8,128)S(1)} %collective-permute-done.5), channel_id=1, source_target_pairs={{0,1},{1,2},{2,3},{3,0},{4,5},{5,6},{6,7},{7,4},{8,9},{9,10},{10,1... | collective-permute-start | bytes 786440 | tf_op jit(solution)/shard_map/ppermute | solution.py:30
  30.1 8.1 %collective-permute-start.1 = (f32[2,128,256]{2,1,0:T(8,128)S(1)}, f32[2,128,256]{2,1,0:T(8,128)S(1)}, u32[]{:S(2)}, u32[]{:S(2)}) collective-permute-start(f32[2,128,256]{2,1,0:T(8,128)S(1)} %collective-permute-done), channel_id=1, source_target_pairs={{0,4},{4,0},{1,5},{5,1},{2,6},{6,2},{3,7},{7,3},{8,12},{12,8},{9,1... | collective-permute-start | bytes 786440 | tf_op jit(solution)/shard_map/ppermute | solution.py:14
  38.3 11.2 %collective-permute-start.2 = (f32[2,128,256]{2,1,0:T(8,128)S(1)}, f32[2,128,256]{2,1,0:T(8,128)S(1)}, u32[]{:S(2)}, u32[]{:S(2)}) collective-permute-start(f32[2,128,256]{2,1,0:T(8,128)S(1)} %get-tuple-element.34), channel_id=1, source_target_pairs={{0,2},{2,0},{1,3},{3,1},{4,6},{6,4},{5,7},{7,5},{8,10},{10,8},{9,1... | collective-permute-start | bytes 786440 | tf_op jit(solution)/shard_map/ppermute | solution.py:14
  49.5 8.2 %collective-permute-start.3 = (f32[2,128,256]{2,1,0:T(8,128)S(1)}, f32[2,128,256]{2,1,0:T(8,128)S(1)}, u32[]{:S(2)}, u32[]{:S(2)}) collective-permute-start(f32[2,128,256]{2,1,0:T(8,128)S(1)} %collective-permute-done.2), channel_id=1, source_target_pairs={{0,8},{8,0},{1,9},{9,1},{2,10},{10,2},{3,11},{11,3},{4,12},{12,4},... | collective-permute-start | bytes 786440 | tf_op jit(solution)/shard_map/ppermute | solution.py:14
Sparse Core Ops, SparseCore 0:
  58.6 25.8 all-gather.1
